TPU v7x, 8 devices: a whole 2x2x1 slice. The times are simulated.
8 devices in a mesh: dp: 1 (over z), a: 2 (over y), b: 4 (over x, core).
Axes of the slice: x: 2, y: 2, z: 1, core: 2. Of those that a mesh axis runs over, the one named last changes fastest.
Arguments:
- x: bfloat16 [2048, 12288], P('dp', ('a', 'b'))
- w_gate: bfloat16 [12288, 28672], P('a', 'b')
- w_up: bfloat16 [12288, 28672], P('a', 'b')
- w_down: bfloat16 [28672, 12288], P('b', 'a')
Outputs:
- output: bfloat16 [2048, 12288], P('dp', ('a', 'b'))
All inputs are finite; a program needn't handle non-finite values.
Results may differ from a plain program's by a relative error of at most 0.016.
Values are sent between devices in bfloat16 or wider.
A program may use at most 2 GiB of HBM per device.

v0:
```python
import jax
import jax.numpy as jnp


def solution(mesh):
    def step(x, w_gate, w_up, w_down):
        gate, up = jnp.dot(x, w_gate), jnp.dot(x, w_up)
        hidden = (jax.nn.silu(gate.astype(jnp.float32)) * up.astype(jnp.float32)).astype(jnp.bfloat16)
        return jnp.dot(hidden, w_down)

    return step
```

profile of v0, /device:TPU:0, one launch (start us, length us, event | category | flops | bytes accessed | tf_op | source)
XLA Modules:
  0.0 2214.1 jit_solution(10893248174672399122)
XLA Ops:
  6.5 0.0 all-gather.4.cloned.1.call-start
  6.5 0.7 all-gather.4.cloned.1.call-update
  7.3 0.0 all-reduce.7.cloned.1.call-start
  7.3 157.3 %all-gather.4.cloned.1.call-done = bf16[2048,6144]{1,0:T(8,128)(2,1)} async-done(((bf16[2048,1536]{1,0:T(8,128)(2,1)}), bf16[2048,6144]{1,0:T(8,128)(2,1)}) %all-gather.4.cloned.1.call-update) | async-done | bytes 25165840 | tf_op args[0]
  164.6 197.1 %fusion.9 = bf16[2048,7168]{1,0:T(8,128)(2,1)} fusion(bf16[2048,6144]{1,0:T(8,128)(2,1)} %all-gather.4.cloned.1.call-done, bf16[6144,7168]{1,0:T(8,128)(2,1)} %param.2), kind=kOutput, calls=%fused_computation.10 | convolution fusion | flops 180388626432 | bytes 142606336 | tf_op jit(solution)/dot_general | solution.py:7
  361.6 197.0 %fusion.8 = bf16[2048,7168]{1,0:T(8,128)(2,1)} fusion(bf16[2048,6144]{1,0:T(8,128)(2,1)} %all-gather.4.cloned.1.call-done, bf16[6144,7168]{1,0:T(8,128)(2,1)} %param.1), kind=kOutput, calls=%fused_computation.9 | convolution fusion | flops 180388626432 | bytes 142606336 | tf_op jit(solution)/dot_general | solution.py:7
  558.6 0.0 all-reduce.7.cloned.1.call-update
  558.6 0.0 reduce-scatter.4.cloned.1.call-start
  558.7 1271.3 %all-reduce.7.cloned.1.call-done = (bf16[2048,7168]{1,0:T(8,128)(2,1)}, bf16[2048,7168]{1,0:T(8,128)(2,1)}) async-done(((bf16[2048,7168]{1,0:T(8,128)(2,1)}, bf16[2048,7168]{1,0:T(8,128)(2,1)}), (bf16[2048,7168]{1,0:T(8,128)(2,1)}, bf16[2048,7168]{1,0:T(8,128)(2,1)})) %all-reduce.7.cloned.1.call-update) | async-done | bytes 58720272 | tf_op jit(solution)/dot_general | solution.py:7
  1830.0 208.0 %fusion.5 = bf16[2048,6144]{1,0:T(8,128)(2,1)} fusion(bf16[7168,6144]{1,0:T(8,128)(2,1)} %param.3, bf16[2048,7168]{1,0:T(8,128)(2,1)} %get-tuple-element.4, bf16[2048,7168]{1,0:T(8,128)(2,1)} %get-tuple-element.5), kind=kOutput, calls=%fused_computation.7 | convolution fusion | flops 180506066944 | bytes 171966464 | tf_op jit(solution)/dot_general | solution.py:9
  2037.9 0.0 reduce-scatter.4.cloned.1.call-update
  2038.0 169.6 %reduce-scatter.4.cloned.1.call-done = bf16[2048,1536]{1,0:T(8,128)(2,1)} async-done(((bf16[2048,6144]{1,0:T(8,128)(2,1)}), bf16[2048,1536]{1,0:T(8,128)(2,1)}) %reduce-scatter.4.cloned.1.call-update) | async-done | bytes 6291472
Async XLA Ops:
  6.5 158.0 %all-gather.4.cloned.1.call-start = ((), (), s32[]{:S(2)}) async-start(), calls=%async_computation.1 | async-start | bytes 31457280 | tf_op args[0]
  7.3 1822.7 %all-reduce.7.cloned.1.call-start = ((), (), s32[]{:S(2)}) async-start(), calls=%async_computation.3 | async-start | bytes 117440512 | tf_op jit(solution)/dot_general | solution.py:7
  558.6 1648.9 %reduce-scatter.4.cloned.1.call-start = ((), (), s32[]{:S(2)}) async-start(), calls=%async_computation.2 | async-start | bytes 31457280
Sparse Core Ops, SparseCore 0:
  8.9 155.6 all-gather.3
  558.8 1271.1 all-reduce.6
  2038.1 169.4 reduce-scatter.3
where the time goes:
time: 2210 us
  waiting for transfers between devices  1600 us (72%)
  matrix products  602 us (27%)
    dot_general x1, waiting for transfers between devices, step(): gate, up = (jnp.dot(x, w_gate), jnp.dot(x, w_up))  1270 us
    dot_general x2, matrix products, step(): gate, up = (jnp.dot(x, w_gate), jnp.dot(x, w_up))  394 us
    unnamed x5, waiting for transfers between devices  328 us
    dot_general x1, matrix products, step(): return jnp.dot(hidden, w_down)  208 us
  transfers between devices with their start and end apart: 3, of which 3 were waited for; matrix products, arithmetic and copies ran while one was open for 0% of the time, Pallas kernels for 0%

commit v1 on v0

v1 whole, which is shorter than its diff:
```python
import jax
import jax.numpy as jnp
from jax import lax
from jax.sharding import PartitionSpec as P

HALVES = (256, 256, 256, 256)


def solution(mesh):
    na, nb = mesh.shape["a"], mesh.shape["b"]
    swap = [(0, 1), (1, 0)]

    def dot(p, q):
        return jnp.dot(p, q, preferred_element_type=jnp.float32)

    def body(x, w_gate, w_up, w_down):
        me = lax.axis_index("a")
        y = jnp.zeros((x.shape[0], w_down.shape[1] // nb), jnp.bfloat16)
        start = 0
        for rows in HALVES:
            mine = start + me * rows
            theirs = start + (1 - me) * rows
            start += 2 * rows
            xt = lax.all_gather(lax.dynamic_slice_in_dim(x, theirs, rows), "b", axis=1, tiled=True)
            gt = lax.ppermute(dot(xt, w_gate).astype(jnp.bfloat16), "a", swap)
            ut = lax.ppermute(dot(xt, w_up).astype(jnp.bfloat16), "a", swap)
            xm = lax.all_gather(lax.dynamic_slice_in_dim(x, mine, rows), "b", axis=1, tiled=True)
            gate = dot(xm, w_gate) + gt.astype(jnp.float32)
            up = dot(xm, w_up) + ut.astype(jnp.float32)
            hm = (jax.nn.silu(gate) * up).astype(jnp.bfloat16)
            ht = lax.ppermute(hm, "a", swap)
            for h, at in ((hm, mine), (ht, theirs)):
                part = dot(h, w_down).astype(jnp.bfloat16)
                out = lax.psum_scatter(part, "b", scatter_dimension=1, tiled=True)
                y = lax.dynamic_update_slice_in_dim(y, out, at, 0)
        return y

    return jax.shard_map(
        body,
        mesh=mesh,
        in_specs=(P("dp", ("a", "b")), P("a", "b"), P("a", "b"), P("b", "a")),
        out_specs=P("dp", ("a", "b")),
        check_vma=False,
    )
```

time: 2210 us -> 1270 us (0.57)
  waiting for transfers between devices: 1600 us -> 308 us
  matrix products: 602 us -> 897 us
  local copies, waits for them, and re-layouts: 0 us -> 24 us
    dot_general x1 -> x0, waiting for transfers between devices: 1270 us -> none  [step(): gate, up = (jnp.dot(x, w_gate), jnp.dot(x, w_up))]
    unnamed x5 -> x16, waiting for transfers between devices: 328 us -> 4.49 us
    dot_general x3 -> x24, matrix products: 602 us -> 897 us  [dot(): return jnp.dot(p, q, preferred_element_type=jnp.float32)]
    ppermute x0 -> x12, waiting for transfers between devices: none -> 264 us  [the longest x4 264 us: body(): ht = lax.ppermute(hm, 'a', swap)]
    all_gather x0 -> x8, waiting for transfers between devices: none -> 23.7 us  [the longest x4 23.7 us: body(): lax.all_gather(lax.dynamic_slice_in_dim(x, theirs, rows), 'b', axis=1, ti...]
  transfers between devices with their start and end apart: 3 -> 28, of which waited for: 3 -> 6; matrix products, arithmetic and copies ran while one was open for 0% -> 73% of each run, Pallas kernels for 0% -> 0%
where the time goes in v1:
time: 1270 us; the launch traced here: 1260 us
  matrix products  897 us (71%)
  waiting for transfers between devices  308 us (24%)
  local copies, waits for them, and re-layouts  24 us (2%)
  starting transfers between devices  14.6 us (1%)
  between operations  13.9 us (1%)
    dot_general x24, matrix products, dot(): return jnp.dot(p, q, preferred_element_type=jnp.float32)  897 us
    ppermute x4, waiting for transfers between devices, body(): ht = lax.ppermute(hm, 'a', swap)  264 us
  transfers between devices with their start and end apart: 28, of which 6 were waited for; matrix products, arithmetic and copies ran while one was open for 73% of the time, Pallas kernels for 0%

profile of v1, /device:TPU:0, one launch (start us, length us, event | category | flops | bytes accessed | tf_op | source)
XLA Modules:
  0.0 1257.2 jit_solution(13767750608528139027)
XLA Ops:
  6.5 5.5 constant_dynamic-slice_fusion
  16.9 23.7 %all-gather.11.cloned.1.call-done = bf16[256,6144]{1,0:T(8,128)(2,1)} async-done(((bf16[256,1536]{1,0:T(8,128)(2,1)}), bf16[256,6144]{1,0:T(8,128)(2,1)}) %all-gather.11.cloned.1.call-update) | async-done | bytes 3145744 | tf_op jit(solution)/shard_map/all_gather | solution.py:24
  40.5 41.5 %convolution_convert_fusion.7 = bf16[256,7168]{1,0:T(8,128)(2,1)} fusion(bf16[256,6144]{1,0:T(8,128)(2,1)} %all-gather.11.cloned.1.call-done, bf16[6144,7168]{1,0:T(8,128)(2,1)} %param.5), kind=kOutput, calls=%fused_computation.7 | convolution fusion | flops 22550413312 | bytes 94896128 | tf_op jit(solution)/shard_map/dot_general | solution.py:14
  82.0 1.5 collective-permute-start
  83.5 35.2 %convolution_convert_fusion.6 = bf16[256,7168]{1,0:T(8,128)(2,1)} fusion(bf16[256,6144]{1,0:T(8,128)(2,1)S(1)} %copy-done.8, bf16[6144,7168]{1,0:T(8,128)(2,1)} %param.6), kind=kOutput, calls=%fused_computation.6 | convolution fusion | flops 22550413312 | bytes 94896128 | tf_op jit(solution)/shard_map/dot_general | solution.py:14
  119.2 41.9 %convolution_convert_fusion.5 = bf16[256,7168]{1,0:T(8,128)(2,1)} fusion(bf16[256,6144]{1,0:T(8,128)(2,1)} %all-gather.15.cloned.1.call-done, bf16[6144,7168]{1,0:T(8,128)(2,1)} %param.5), kind=kOutput, calls=%fused_computation.5 | convolution fusion | flops 22550413312 | bytes 94896128 | tf_op jit(solution)/shard_map/dot_general | solution.py:14
  161.1 1.5 collective-permute-start.3
  162.6 35.3 %convolution_convert_fusion.4 = bf16[256,7168]{1,0:T(8,128)(2,1)} fusion(bf16[256,6144]{1,0:T(8,128)(2,1)S(1)} %copy-done.7, bf16[6144,7168]{1,0:T(8,128)(2,1)} %param.6), kind=kOutput, calls=%fused_computation.4 | convolution fusion | flops 22550413312 | bytes 94896128 | tf_op jit(solution)/shard_map/dot_general | solution.py:14
  198.4 41.6 %convolution_convert_fusion.3 = bf16[256,7168]{1,0:T(8,128)(2,1)} fusion(bf16[256,6144]{1,0:T(8,128)(2,1)} %all-gather.19.cloned.1.call-done, bf16[6144,7168]{1,0:T(8,128)(2,1)} %param.5), kind=kOutput, calls=%fused_computation.3 | convolution fusion | flops 22550413312 | bytes 94896128 | tf_op jit(solution)/shard_map/dot_general | solution.py:14
  240.1 1.5 collective-permute-start.6
  241.5 35.2 %convolution_convert_fusion.2 = bf16[256,7168]{1,0:T(8,128)(2,1)} fusion(bf16[256,6144]{1,0:T(8,128)(2,1)S(1)} %copy-done.5, bf16[6144,7168]{1,0:T(8,128)(2,1)} %param.6), kind=kOutput, calls=%fused_computation.2 | convolution fusion | flops 22550413312 | bytes 94896128 | tf_op jit(solution)/shard_map/dot_general | solution.py:14
  276.8 42.0 %convolution_convert_fusion = bf16[256,7168]{1,0:T(8,128)(2,1)} fusion(bf16[256,6144]{1,0:T(8,128)(2,1)} %all-gather.23.cloned.1.call-done, bf16[6144,7168]{1,0:T(8,128)(2,1)} %param.6), kind=kOutput, calls=%fused_computation | convolution fusion | flops 22550413312 | bytes 94896128 | tf_op jit(solution)/shard_map/dot_general | solution.py:14
  318.8 35.2 %convolution_convert_fusion.1 = bf16[256,7168]{1,0:T(8,128)(2,1)} fusion(bf16[256,6144]{1,0:T(8,128)(2,1)S(1)} %copy-done.6, bf16[6144,7168]{1,0:T(8,128)(2,1)} %param.5), kind=kOutput, calls=%fused_computation.1 | convolution fusion | flops 22550413312 | bytes 94896128 | tf_op jit(solution)/shard_map/dot_general | solution.py:14
  354.0 42.8 %fusion = f32[256,7168]{1,0:T(8,128)} fusion(bf16[256,6144]{1,0:T(8,128)(2,1)} %all-gather.9.cloned.1.call-done, bf16[6144,7168]{1,0:T(8,128)(2,1)} %param.5), kind=kOutput, calls=%fused_computation.36 | convolution fusion | flops 22548578304 | bytes 98566144 | tf_op jit(solution)/shard_map/dot_general | solution.py:14
  397.4 38.3 %multiply_convert_fusion.3 = bf16[256,7168]{1,0:T(8,128)(2,1)} fusion(bf16[256,7168]{1,0:T(8,128)(2,1)} %collective-permute-done.1, f32[256,7168]{1,0:T(8,128)} %fusion, bf16[256,7168]{1,0:T(8,128)(2,1)} %collective-permute-done, bf16[256,6144]{1,0:T(8,128)(2,1)S(1)} %copy-done.4, bf16[6144,7168]{1,0:T(8,128)(2,1)} %param.6), kind=kOutput, calls=%fused_computation.19 | convolution fusion | flops 22566928384 | bytes 109576192 | tf_op jit(solution)/shard_map/dot_general | solution.py:14
  435.7 1.5 collective-permute-start.2
  437.2 35.5 %convolution_convert_fusion.15 = bf16[256,6144]{1,0:T(8,128)(2,1)} fusion(bf16[256,7168]{1,0:T(8,128)(2,1)} %multiply_convert_fusion.3, bf16[7168,6144]{1,0:T(8,128)(2,1)} %param.7), kind=kOutput, calls=%fused_computation.15 | convolution fusion | flops 22550151168 | bytes 94896128 | tf_op jit(solution)/shard_map/dot_general | solution.py:14
  472.8 36.2 %fusion.1 = f32[256,7168]{1,0:T(8,128)} fusion(bf16[256,6144]{1,0:T(8,128)(2,1)} %all-gather.13.cloned.1.call-done, bf16[6144,7168]{1,0:T(8,128)(2,1)} %param.5), kind=kOutput, calls=%fused_computation.37 | convolution fusion | flops 22548578304 | bytes 98566144 | tf_op jit(solution)/shard_map/dot_general | solution.py:14
  509.0 126.3 %collective-permute-done.2 = bf16[256,7168]{1,0:T(8,128)(2,1)} collective-permute-done((bf16[256,7168]{1,0:T(8,128)(2,1)}, bf16[256,7168]{1,0:T(8,128)(2,1)}, u32[]{:S(2)}, u32[]{:S(2)}) %collective-permute-start.2) | collective-permute-done | bytes 3670048 | tf_op jit(solution)/shard_map/ppermute | solution.py:31
  635.4 1.5 collective-permute-start.10
  636.8 35.3 %convolution_convert_fusion.14 = bf16[256,6144]{1,0:T(8,128)(2,1)} fusion(bf16[256,7168]{1,0:T(8,128)(2,1)} %collective-permute-done.2, bf16[7168,6144]{1,0:T(8,128)(2,1)} %param.7), kind=kOutput, calls=%fused_computation.14 | convolution fusion | flops 22550151168 | bytes 94896128 | tf_op jit(solution)/shard_map/dot_general | solution.py:14
  672.8 38.5 %multiply_convert_fusion.2 = bf16[256,7168]{1,0:T(8,128)(2,1)} fusion(bf16[256,7168]{1,0:T(8,128)(2,1)} %collective-permute-done.4, f32[256,7168]{1,0:T(8,128)} %fusion.1, bf16[256,7168]{1,0:T(8,128)(2,1)} %collective-permute-done.3, bf16[256,6144]{1,0:T(8,128)(2,1)S(1)} %copy-done.3, bf16[6144,7168]{1,0:T(8,128)(2,1)} %param.6), kind=kOutput, calls=%fused_computation.18 | convolution fusion | flops 22566928384 | bytes 109576192 | tf_op jit(solution)/shard_map/dot_general | solution.py:14
  711.3 1.5 collective-permute-start.5
  712.8 35.4 %convolution_convert_fusion.13 = bf16[256,6144]{1,0:T(8,128)(2,1)} fusion(bf16[256,7168]{1,0:T(8,128)(2,1)} %multiply_convert_fusion.2, bf16[7168,6144]{1,0:T(8,128)(2,1)} %param.7), kind=kOutput, calls=%fused_computation.13 | convolution fusion | flops 22550151168 | bytes 94896128 | tf_op jit(solution)/shard_map/dot_general | solution.py:14
  748.3 36.6 %fusion.2 = f32[256,7168]{1,0:T(8,128)} fusion(bf16[256,6144]{1,0:T(8,128)(2,1)} %all-gather.17.cloned.1.call-done, bf16[6144,7168]{1,0:T(8,128)(2,1)} %param.5), kind=kOutput, calls=%fused_computation.38 | convolution fusion | flops 22548578304 | bytes 98566144 | tf_op jit(solution)/shard_map/dot_general | solution.py:14
  784.9 88.5 %collective-permute-done.5 = bf16[256,7168]{1,0:T(8,128)(2,1)} collective-permute-done((bf16[256,7168]{1,0:T(8,128)(2,1)}, bf16[256,7168]{1,0:T(8,128)(2,1)}, u32[]{:S(2)}, u32[]{:S(2)}) %collective-permute-start.5) | collective-permute-done | bytes 3670048 | tf_op jit(solution)/shard_map/ppermute | solution.py:31
  873.4 35.3 %convolution_convert_fusion.12 = bf16[256,6144]{1,0:T(8,128)(2,1)} fusion(bf16[256,7168]{1,0:T(8,128)(2,1)} %collective-permute-done.5, bf16[7168,6144]{1,0:T(8,128)(2,1)} %param.7), kind=kOutput, calls=%fused_computation.12 | convolution fusion | flops 22550151168 | bytes 94896128 | tf_op jit(solution)/shard_map/dot_general | solution.py:14
  908.8 38.5 %multiply_convert_fusion.1 = bf16[256,7168]{1,0:T(8,128)(2,1)} fusion(bf16[256,7168]{1,0:T(8,128)(2,1)} %collective-permute-done.7, f32[256,7168]{1,0:T(8,128)} %fusion.2, bf16[256,7168]{1,0:T(8,128)(2,1)} %collective-permute-done.6, bf16[256,6144]{1,0:T(8,128)(2,1)S(1)} %copy-done.2, bf16[6144,7168]{1,0:T(8,128)(2,1)} %param.6), kind=kOutput, calls=%fused_computation.17 | convolution fusion | flops 22566928384 | bytes 109576192 | tf_op jit(solution)/shard_map/dot_general | solution.py:14
  947.3 1.5 collective-permute-start.8
  948.7 35.4 %convolution_convert_fusion.11 = bf16[256,6144]{1,0:T(8,128)(2,1)} fusion(bf16[256,7168]{1,0:T(8,128)(2,1)} %multiply_convert_fusion.1, bf16[7168,6144]{1,0:T(8,128)(2,1)} %param.7), kind=kOutput, calls=%fused_computation.11 | convolution fusion | flops 22550151168 | bytes 94896128 | tf_op jit(solution)/shard_map/dot_general | solution.py:14
  984.2 36.5 %fusion.3 = f32[256,7168]{1,0:T(8,128)} fusion(bf16[256,6144]{1,0:T(8,128)(2,1)} %all-gather.21.cloned.1.call-done, bf16[6144,7168]{1,0:T(8,128)(2,1)} %param.5), kind=kOutput, calls=%fused_computation.39 | convolution fusion | flops 22548578304 | bytes 98566144 | tf_op jit(solution)/shard_map/dot_general | solution.py:14
  1020.7 6.6 collective-permute-done.8
  1027.2 35.3 %convolution_convert_fusion.10 = bf16[256,6144]{1,0:T(8,128)(2,1)} fusion(bf16[256,7168]{1,0:T(8,128)(2,1)} %collective-permute-done.8, bf16[7168,6144]{1,0:T(8,128)(2,1)} %param.7), kind=kOutput, calls=%fused_computation.10 | convolution fusion | flops 22550151168 | bytes 94896128 | tf_op jit(solution)/shard_map/dot_general | solution.py:14
  1062.6 38.6 %multiply_convert_fusion = bf16[256,7168]{1,0:T(8,128)(2,1)} fusion(bf16[256,7168]{1,0:T(8,128)(2,1)} %collective-permute-done.10, f32[256,7168]{1,0:T(8,128)} %fusion.3, bf16[256,7168]{1,0:T(8,128)(2,1)} %collective-permute-done.9, bf16[256,6144]{1,0:T(8,128)(2,1)S(1)} %copy-done.1, bf16[6144,7168]{1,0:T(8,128)(2,1)} %param.6), kind=kOutput, calls=%fused_computation.16 | convolution fusion | flops 22566928384 | bytes 109576192 | tf_op jit(solution)/shard_map/dot_general | solution.py:14
  1101.2 1.5 collective-permute-start.11
  1102.7 35.4 %convolution_convert_fusion.9 = bf16[256,6144]{1,0:T(8,128)(2,1)} fusion(bf16[256,7168]{1,0:T(8,128)(2,1)} %multiply_convert_fusion, bf16[7168,6144]{1,0:T(8,128)(2,1)} %param.7), kind=kOutput, calls=%fused_computation.9 | convolution fusion | flops 22550151168 | bytes 94896128 | tf_op jit(solution)/shard_map/dot_general | solution.py:14
  1138.1 42.3 %collective-permute-done.11 = bf16[256,7168]{1,0:T(8,128)(2,1)} collective-permute-done((bf16[256,7168]{1,0:T(8,128)(2,1)}, bf16[256,7168]{1,0:T(8,128)(2,1)}, u32[]{:S(2)}, u32[]{:S(2)}) %collective-permute-start.11) | collective-permute-done | bytes 3670048 | tf_op jit(solution)/shard_map/ppermute | solution.py:31
  1180.4 35.6 %convolution_convert_fusion.8 = bf16[256,6144]{1,0:T(8,128)(2,1)} fusion(bf16[256,7168]{1,0:T(8,128)(2,1)} %collective-permute-done.11, bf16[7168,6144]{1,0:T(8,128)(2,1)} %param.7), kind=kOutput, calls=%fused_computation.8 | convolution fusion | flops 22550151168 | bytes 94896128 | tf_op jit(solution)/shard_map/dot_general | solution.py:14
  1216.1 3.1 broadcast_in_dim.3
  1219.2 0.9 constant_dynamic-update-slice_fusion.7
  1220.1 2.1 constant_dynamic-update-slice_fusion.6
  1222.2 2.1 constant_dynamic-update-slice_fusion.5
  1224.3 2.1 constant_dynamic-update-slice_fusion.4
  1226.3 2.1 constant_dynamic-update-slice_fusion.3
  1228.4 2.1 constant_dynamic-update-slice_fusion.2
  1230.5 2.1 constant_dynamic-update-slice_fusion.1
  1232.5 15.6 %reduce-scatter.23.cloned.1.call-done = bf16[256,1536]{1,0:T(8,128)(2,1)} async-done(((bf16[256,6144]{1,0:T(8,128)(2,1)}), bf16[256,1536]{1,0:T(8,128)(2,1)}) %reduce-scatter.23.cloned.1.call-update) | async-done | bytes 786448 | tf_op jit(solution)/shard_map/reduce_scatter | solution.py:34
  1248.2 2.1 constant_dynamic-update-slice_fusion
  (76 shorter events, 7.5 us)
Async XLA Ops:
  6.5 34.0 %all-gather.11.cloned.1.call-start = ((), (), s32[]{:S(2)}) async-start(), calls=%async_computation.9 | async-start | bytes 3932160 | tf_op jit(solution)/shard_map/all_gather | solution.py:24
  12.1 107.1 %all-gather.15.cloned.1.call-start = ((), (), s32[]{:S(2)}) async-start(), calls=%async_computation.13 | async-start | bytes 3932160 | tf_op jit(solution)/shard_map/all_gather | solution.py:24
  12.8 185.6 %all-gather.19.cloned.1.call-start = ((), (), s32[]{:S(2)}) async-start(), calls=%async_computation.17 | async-start | bytes 3932160 | tf_op jit(solution)/shard_map/all_gather | solution.py:24
  13.6 263.2 %all-gather.23.cloned.1.call-start = ((), (), s32[]{:S(2)}) async-start(), calls=%async_computation.21 | async-start | bytes 3932160 | tf_op jit(solution)/shard_map/all_gather | solution.py:24
  14.2 339.8 %all-gather.9.cloned.1.call-start = ((), (), s32[]{:S(2)}) async-start(), calls=%async_computation.8 | async-start | bytes 3932160 | tf_op jit(solution)/shard_map/all_gather | solution.py:27
  14.7 458.1 %all-gather.13.cloned.1.call-start = ((), (), s32[]{:S(2)}) async-start(), calls=%async_computation.12 | async-start | bytes 3932160 | tf_op jit(solution)/shard_map/all_gather | solution.py:27
  15.3 732.9 %all-gather.17.cloned.1.call-start = ((), (), s32[]{:S(2)}) async-start(), calls=%async_computation.16 | async-start | bytes 3932160 | tf_op jit(solution)/shard_map/all_gather | solution.py:27
  16.1 968.1 %all-gather.21.cloned.1.call-start = ((), (), s32[]{:S(2)}) async-start(), calls=%async_computation.20 | async-start | bytes 3932160 | tf_op jit(solution)/shard_map/all_gather | solution.py:27
  16.8 1199.2 %reduce-scatter.9.cloned.1.call-start = ((), (), s32[]{:S(2)}) async-start(), calls=%async_computation.10 | async-start | bytes 3932160 | tf_op jit(solution)/shard_map/reduce_scatter | solution.py:34
  40.5 42.9 %copy-start.8 = (bf16[256,6144]{1,0:T(8,128)(2,1)S(1)}, bf16[256,6144]{1,0:T(8,128)(2,1)}, u32[]{:S(2)}) copy-start(bf16[256,6144]{1,0:T(8,128)(2,1)} %all-gather.11.cloned.1.call-done) | copy-start | bytes 9437188
  82.0 314.8 %collective-permute-start = (bf16[256,7168]{1,0:T(8,128)(2,1)}, bf16[256,7168]{1,0:T(8,128)(2,1)}, u32[]{:S(2)}, u32[]{:S(2)}) collective-permute-start(bf16[256,7168]{1,0:T(8,128)(2,1)} %convolution_convert_fusion.7), channel_id=1, source_target_pairs={{0,4},{4,0},{1,5},{5,1},{2,6},{6,2},{3,7},{7,3}} | collective-permute-start | bytes 11010056 | tf_op jit(solution)/shard_map/ppermute | solution.py:25
  118.7 278.7 %collective-permute-start.1 = (bf16[256,7168]{1,0:T(8,128)(2,1)}, bf16[256,7168]{1,0:T(8,128)(2,1)}, u32[]{:S(2)}, u32[]{:S(2)}) collective-permute-start(bf16[256,7168]{1,0:T(8,128)(2,1)} %convolution_convert_fusion.6), channel_id=1, source_target_pairs={{0,4},{4,0},{1,5},{5,1},{2,6},{6,2},{3,7},{7,3}} | collective-permute-start | bytes 11010056 | tf_op jit(solution)/shard_map/ppermute | solution.py:26
  119.2 43.4 %copy-start.7 = (bf16[256,6144]{1,0:T(8,128)(2,1)S(1)}, bf16[256,6144]{1,0:T(8,128)(2,1)}, u32[]{:S(2)}) copy-start(bf16[256,6144]{1,0:T(8,128)(2,1)} %all-gather.15.cloned.1.call-done) | copy-start | bytes 9437188
  161.1 511.1 %collective-permute-start.3 = (bf16[256,7168]{1,0:T(8,128)(2,1)}, bf16[256,7168]{1,0:T(8,128)(2,1)}, u32[]{:S(2)}, u32[]{:S(2)}) collective-permute-start(bf16[256,7168]{1,0:T(8,128)(2,1)} %convolution_convert_fusion.5), channel_id=1, source_target_pairs={{0,4},{4,0},{1,5},{5,1},{2,6},{6,2},{3,7},{7,3}} | collective-permute-start | bytes 11010056 | tf_op jit(solution)/shard_map/ppermute | solution.py:25
  197.9 475.0 %collective-permute-start.4 = (bf16[256,7168]{1,0:T(8,128)(2,1)}, bf16[256,7168]{1,0:T(8,128)(2,1)}, u32[]{:S(2)}, u32[]{:S(2)}) collective-permute-start(bf16[256,7168]{1,0:T(8,128)(2,1)} %convolution_convert_fusion.4), channel_id=1, source_target_pairs={{0,4},{4,0},{1,5},{5,1},{2,6},{6,2},{3,7},{7,3}} | collective-permute-start | bytes 11010056 | tf_op jit(solution)/shard_map/ppermute | solution.py:26
  198.4 43.1 %copy-start.5 = (bf16[256,6144]{1,0:T(8,128)(2,1)S(1)}, bf16[256,6144]{1,0:T(8,128)(2,1)}, u32[]{:S(2)}) copy-start(bf16[256,6144]{1,0:T(8,128)(2,1)} %all-gather.19.cloned.1.call-done) | copy-start | bytes 9437188
  240.1 668.7 %collective-permute-start.6 = (bf16[256,7168]{1,0:T(8,128)(2,1)}, bf16[256,7168]{1,0:T(8,128)(2,1)}, u32[]{:S(2)}, u32[]{:S(2)}) collective-permute-start(bf16[256,7168]{1,0:T(8,128)(2,1)} %convolution_convert_fusion.3), channel_id=1, source_target_pairs={{0,4},{4,0},{1,5},{5,1},{2,6},{6,2},{3,7},{7,3}} | collective-permute-start | bytes 11010056 | tf_op jit(solution)/shard_map/ppermute | solution.py:25
  276.7 42.0 %copy-start.6 = (bf16[256,6144]{1,0:T(8,128)(2,1)S(1)}, bf16[256,6144]{1,0:T(8,128)(2,1)}, u32[]{:S(2)}) copy-start(bf16[256,6144]{1,0:T(8,128)(2,1)} %all-gather.23.cloned.1.call-done) | copy-start | bytes 9437188
  354.0 43.4 %copy-start.4 = (bf16[256,6144]{1,0:T(8,128)(2,1)S(1)}, bf16[256,6144]{1,0:T(8,128)(2,1)}, u32[]{:S(2)}) copy-start(bf16[256,6144]{1,0:T(8,128)(2,1)} %all-gather.9.cloned.1.call-done) | copy-start | bytes 9437188
  396.8 511.9 %collective-permute-start.7 = (bf16[256,7168]{1,0:T(8,128)(2,1)}, bf16[256,7168]{1,0:T(8,128)(2,1)}, u32[]{:S(2)}, u32[]{:S(2)}) collective-permute-start(bf16[256,7168]{1,0:T(8,128)(2,1)} %convolution_convert_fusion.2), channel_id=1, source_target_pairs={{0,4},{4,0},{1,5},{5,1},{2,6},{6,2},{3,7},{7,3}} | collective-permute-start | bytes 11010056 | tf_op jit(solution)/shard_map/ppermute | solution.py:26
  435.7 199.7 %collective-permute-start.2 = (bf16[256,7168]{1,0:T(8,128)(2,1)}, bf16[256,7168]{1,0:T(8,128)(2,1)}, u32[]{:S(2)}, u32[]{:S(2)}) collective-permute-start(bf16[256,7168]{1,0:T(8,128)(2,1)} %multiply_convert_fusion.3), channel_id=1, source_target_pairs={{0,4},{4,0},{1,5},{5,1},{2,6},{6,2},{3,7},{7,3}} | collective-permute-start | bytes 11010056 | tf_op jit(solution)/shard_map/ppermute | solution.py:31
  472.7 747.4 %reduce-scatter.11.cloned.1.call-start = ((), (), s32[]{:S(2)}) async-start(), calls=%async_computation.11 | async-start | bytes 3932160 | tf_op jit(solution)/shard_map/reduce_scatter | solution.py:34
  509.0 163.8 %copy-start.3 = (bf16[256,6144]{1,0:T(8,128)(2,1)S(1)}, bf16[256,6144]{1,0:T(8,128)(2,1)}, u32[]{:S(2)}) copy-start(bf16[256,6144]{1,0:T(8,128)(2,1)} %all-gather.13.cloned.1.call-done) | copy-start | bytes 9437188
  635.4 427.2 %collective-permute-start.10 = (bf16[256,7168]{1,0:T(8,128)(2,1)}, bf16[256,7168]{1,0:T(8,128)(2,1)}, u32[]{:S(2)}, u32[]{:S(2)}) collective-permute-start(bf16[256,7168]{1,0:T(8,128)(2,1)} %convolution_convert_fusion), channel_id=1, source_target_pairs={{0,4},{4,0},{1,5},{5,1},{2,6},{6,2},{3,7},{7,3}} | collective-permute-start | bytes 11010056 | tf_op jit(solution)/shard_map/ppermute | solution.py:26
  672.2 550.0 %reduce-scatter.13.cloned.1.call-start = ((), (), s32[]{:S(2)}) async-start(), calls=%async_computation.14 | async-start | bytes 3932160 | tf_op jit(solution)/shard_map/reduce_scatter | solution.py:34
  672.2 390.4 %collective-permute-start.9 = (bf16[256,7168]{1,0:T(8,128)(2,1)}, bf16[256,7168]{1,0:T(8,128)(2,1)}, u32[]{:S(2)}, u32[]{:S(2)}) collective-permute-start(bf16[256,7168]{1,0:T(8,128)(2,1)} %convolution_convert_fusion.1), channel_id=1, source_target_pairs={{0,4},{4,0},{1,5},{5,1},{2,6},{6,2},{3,7},{7,3}} | collective-permute-start | bytes 11010056 | tf_op jit(solution)/shard_map/ppermute | solution.py:25
  711.3 162.1 %collective-permute-start.5 = (bf16[256,7168]{1,0:T(8,128)(2,1)}, bf16[256,7168]{1,0:T(8,128)(2,1)}, u32[]{:S(2)}, u32[]{:S(2)}) collective-permute-start(bf16[256,7168]{1,0:T(8,128)(2,1)} %multiply_convert_fusion.2), channel_id=1, source_target_pairs={{0,4},{4,0},{1,5},{5,1},{2,6},{6,2},{3,7},{7,3}} | collective-permute-start | bytes 11010056 | tf_op jit(solution)/shard_map/ppermute | solution.py:31
  748.2 476.1 %reduce-scatter.15.cloned.1.call-start = ((), (), s32[]{:S(2)}) async-start(), calls=%async_computation.15 | async-start | bytes 3932160 | tf_op jit(solution)/shard_map/reduce_scatter | solution.py:34
  784.9 123.8 %copy-start.2 = (bf16[256,6144]{1,0:T(8,128)(2,1)S(1)}, bf16[256,6144]{1,0:T(8,128)(2,1)}, u32[]{:S(2)}) copy-start(bf16[256,6144]{1,0:T(8,128)(2,1)} %all-gather.17.cloned.1.call-done) | copy-start | bytes 9437188
  908.7 317.6 %reduce-scatter.17.cloned.1.call-start = ((), (), s32[]{:S(2)}) async-start(), calls=%async_computation.18 | async-start | bytes 3932160 | tf_op jit(solution)/shard_map/reduce_scatter | solution.py:34
  947.3 80.0 %collective-permute-start.8 = (bf16[256,7168]{1,0:T(8,128)(2,1)}, bf16[256,7168]{1,0:T(8,128)(2,1)}, u32[]{:S(2)}, u32[]{:S(2)}) collective-permute-start(bf16[256,7168]{1,0:T(8,128)(2,1)} %multiply_convert_fusion.1), channel_id=1, source_target_pairs={{0,4},{4,0},{1,5},{5,1},{2,6},{6,2},{3,7},{7,3}} | collective-permute-start | bytes 11010056 | tf_op jit(solution)/shard_map/ppermute | solution.py:31
  984.1 244.3 %reduce-scatter.19.cloned.1.call-start = ((), (), s32[]{:S(2)}) async-start(), calls=%async_computation.19 | async-start | bytes 3932160 | tf_op jit(solution)/shard_map/reduce_scatter | solution.py:34
  1020.7 41.9 %copy-start.1 = (bf16[256,6144]{1,0:T(8,128)(2,1)S(1)}, bf16[256,6144]{1,0:T(8,128)(2,1)}, u32[]{:S(2)}) copy-start(bf16[256,6144]{1,0:T(8,128)(2,1)} %all-gather.21.cloned.1.call-done) | copy-start | bytes 9437188
  1062.5 167.9 %reduce-scatter.21.cloned.1.call-start = ((), (), s32[]{:S(2)}) async-start(), calls=%async_computation.22 | async-start | bytes 3932160 | tf_op jit(solution)/shard_map/reduce_scatter | solution.py:34
  1101.2 79.2 %collective-permute-start.11 = (bf16[256,7168]{1,0:T(8,128)(2,1)}, bf16[256,7168]{1,0:T(8,128)(2,1)}, u32[]{:S(2)}, u32[]{:S(2)}) collective-permute-start(bf16[256,7168]{1,0:T(8,128)(2,1)} %multiply_convert_fusion), channel_id=1, source_target_pairs={{0,4},{4,0},{1,5},{5,1},{2,6},{6,2},{3,7},{7,3}} | collective-permute-start | bytes 11010056 | tf_op jit(solution)/shard_map/ppermute | solution.py:31
  1138.1 110.1 %reduce-scatter.23.cloned.1.call-start = ((), (), s32[]{:S(2)}) async-start(), calls=%async_computation.23 | async-start | bytes 3932160 | tf_op jit(solution)/shard_map/reduce_scatter | solution.py:34
  1216.1 3.1 copy-start
Sparse Core Ops, SparseCore 0:
  12.2 28.2 all-gather.10
  42.1 25.4 all-gather.14
  69.1 25.4 all-gather.18
  96.0 25.4 all-gather.22
  122.8 25.4 all-gather.8
  149.7 25.4 all-gather.12
  176.7 25.4 all-gather.16
  203.8 25.4 all-gather.20
  472.9 31.0 reduce-scatter.8
  672.3 30.9 reduce-scatter.10
  748.3 30.9 reduce-scatter.12
  908.8 31.9 reduce-scatter.14
  984.2 30.9 reduce-scatter.16
  1062.7 31.9 reduce-scatter.18
  1138.2 30.9 reduce-scatter.20
  1216.2 31.9 reduce-scatter.22

commit v2 on v0

v2 whole, which is shorter than its diff:
```python
import jax
import jax.numpy as jnp
from jax import lax
from jax.experimental import pallas as pl
from jax.experimental.pallas import tpu as pltpu
from jax.sharding import PartitionSpec as P

MESH = pl.DeviceIdType.MESH
BF16, F32 = jnp.bfloat16, jnp.float32

HALVES = (128, 448, 288, 160)
TN = 512
HT = TN // 2
NW = 5
RB = 32
ORDER = ("T0", "T1", "T2", "T3", "M0", "M1", "m0", "m1", "M2", "m2", "M3", "m3", "t0", "t1", "t2", "t3")


def solution(mesh):
    def body(x, w_gate, w_up, w_down):
        rows, dx = x.shape
        dk, ff = w_gate.shape
        dn = w_down.shape[1]
        steps, dsteps, groups = ff // HT, dn // TN, ff // TN
        per = dx // TN
        chunks, top = len(HALVES), max(HALVES)
        starts = [2 * sum(HALVES[:c]) for c in range(chunks)]
        plan = [(o[0], int(o[1])) for o in ORDER]
        jobs = [o for o in plan if o[0] in "tm"]
        tiles = [steps if kind in "TM" else dsteps for kind, _ in plan]
        base = [sum(tiles[:i]) for i in range(len(plan))]

        def kernel(x_ref, wg_ref, wu_ref, wd_ref, out_ref, xg_ref, *refs):
            ssend, srecv, hmine, htheirs = (refs[i * chunks : (i + 1) * chunks] for i in range(4))
            yrecv = refs[4 * chunks : 4 * chunks + len(jobs)]
            (lhs, w, gu, so, si, ho, ysend, ystash, yin, yout,
             wsem, lsem, osem, isem, ysem, yosem,
             fw_sem, xs_sem, xr_sem, ss_sem, sr_sem, hs_sem, hr_sem, ys_sem, yr_sem) = refs[4 * chunks + len(jobs) :]
            a, b = lax.axis_index("a"), lax.axis_index("b")
            other = 1 - a
            chip, core = b // 2, lax.rem(b, 2)

            def mate(g):
                flip_chip = 1 - g // 2
                flip_core = lax.rem((g + 1) // 2, 2)
                return 2 * (chip + flip_chip * (1 - 2 * chip)) + core + flip_core * (1 - 2 * core)

            mates = [mate(jnp.int32(g)) for g in range(3)]

            def row(c, mine):
                return pl.multiple_of(starts[c] + (a if mine else other) * HALVES[c], RB)

            def columns(of):
                return pl.ds(pl.multiple_of(of * dx, 128), dx)

            def gate_up_weights(j, slot):
                at = pl.ds(pl.multiple_of(j * HT, HT), HT)
                return (
                    pltpu.make_async_copy(wg_ref.at[:, at], w.at[slot, :dk, :HT], wsem.at[0, slot]),
                    pltpu.make_async_copy(wu_ref.at[:, at], w.at[slot, :dk, HT:], wsem.at[1, slot]),
                )

            def down_weights(j, slot):
                tile = mate(j // per) * per + lax.rem(j, per)
                at = pl.ds(pl.multiple_of(tile * TN, TN), TN)
                return (pltpu.make_async_copy(wd_ref.at[:, at], w.at[slot], wsem.at[0, slot]),)

            def weights(i, j, slot):
                return (gate_up_weights if plan[i][0] in "TM" else down_weights)(j, slot)

            def prefetch(i, j):
                ahead = j + NW - 1
                slot = lax.rem(base[i] + ahead, NW)

                @pl.when(ahead < tiles[i])
                def _():
                    for copy in weights(i, ahead, slot):
                        copy.start()

                if i + 1 < len(plan):
                    @pl.when(ahead >= tiles[i])
                    def _():
                        for copy in weights(i + 1, ahead - tiles[i], slot):
                            copy.start()

            for first in range(NW - 1):
                for copy in weights(0, jnp.int32(first), first):
                    copy.start()

            barrier = pltpu.get_barrier_semaphore()
            for g in range(3):
                pl.semaphore_signal(barrier, inc=1, device_id={"b": mates[g]}, device_id_type=MESH)
            pl.semaphore_signal(barrier, inc=1, device_id={"a": other}, device_id_type=MESH)
            pl.semaphore_wait(barrier, 4)

            def gather(c, mine, g):
                at = pl.ds(row(c, mine), HALVES[c])
                return pltpu.make_async_remote_copy(
                    x_ref.at[at], xg_ref.at[g, at], xs_sem.at[g], xr_sem.at[g, c, int(mine)],
                    device_id={"b": mates[g]}, device_id_type=MESH,
                )

            def forward(c):
                at = pl.ds(row(c, False), HALVES[c])
                return pltpu.make_async_remote_copy(
                    xg_ref.at[0, at], xg_ref.at[1, at], fw_sem, xr_sem.at[1, c, 0],
                    device_id={"b": mates[2]}, device_id_type=MESH,
                )

            for kind, c in plan:
                if kind in "TM":
                    for g in range(3):
                        if (kind, c, g) != ("T", 0, 1):
                            gather(c, kind == "M", g).start()
            gather(0, False, 0).wait_recv()
            forward(0).start()

            def load_x(c, mine):
                r, at = HALVES[c], pl.ds(row(c, mine), HALVES[c])
                copies = [pltpu.make_async_copy(x_ref.at[at], lhs.at[:r, columns(b)], lsem.at[3])]
                copies[0].start()
                for g in (0, 2, 1):
                    if (c, mine, g) != (0, False, 0):
                        gather(c, mine, g).wait_recv()
                    copies.append(pltpu.make_async_copy(xg_ref.at[g, at], lhs.at[:r, columns(mates[g])], lsem.at[g]))
                    copies[-1].start()
                for copy in copies:
                    copy.wait()

            def send_partial(c, g):
                at = pl.ds(2 * g, 2)
                return pltpu.make_async_remote_copy(
                    ssend[c].at[at], srecv[c].at[at], ss_sem.at[c], sr_sem.at[c, g],
                    device_id={"a": other}, device_id_type=MESH,
                )

            def send_hidden(c, g):
                return pltpu.make_async_remote_copy(
                    hmine[c].at[g], htheirs[c].at[g], hs_sem.at[c], hr_sem.at[c, g],
                    device_id={"a": other}, device_id_type=MESH,
                )

            def gate_up(i, c, mine):
                r = HALVES[c]
                load_x(c, mine)
                send = send_hidden if mine else send_partial

                def partial_in(j, slot):
                    return pltpu.make_async_copy(srecv[c].at[j], si.at[slot, :r], isem.at[slot])

                def put(j):
                    slot = lax.rem(j, 2)
                    if mine:
                        at = pl.ds(pl.multiple_of(slot * HT, HT), HT)
                        return pltpu.make_async_copy(ho.at[slot, :r], hmine[c].at[j // 2, :, at], osem.at[slot])
                    return pltpu.make_async_copy(so.at[slot, :r], ssend[c].at[j], osem.at[slot])

                if mine:
                    send_partial(c, 0).wait_recv()
                    partial_in(0, 0).start()

                def step(j, carry):
                    slot, two = lax.rem(base[i] + j, NW), lax.rem(j, 2)
                    prefetch(i, j)
                    if mine:
                        @pl.when(j + 1 < steps)
                        def _():
                            @pl.when(two == 1)
                            def _():
                                send_partial(c, (j + 1) // 2).wait_recv()
                            partial_in(j + 1, 1 - two).start()
                    for copy in weights(i, j, slot):
                        copy.wait()
                    both = jnp.dot(lhs[:r, :dk], w[slot, :dk], preferred_element_type=F32)
                    if mine:
                        gu[:r] = both
                        partial_in(j, two).wait()

                        def block(n, carry):
                            at = pl.ds(pl.multiple_of(n * RB, RB), RB)
                            gate = gu[at, :HT] + si[two, at, :HT].astype(F32)
                            up = gu[at, HT:] + si[two, at, HT:].astype(F32)
                            ho[two, at] = (jax.nn.silu(gate) * up).astype(BF16)
                            return carry

                        lax.fori_loop(0, r // RB, block, 0)
                    else:
                        so[two, :r] = both.astype(BF16)

                    @pl.when(j > 0)
                    def _():
                        put(j - 1).wait()

                        @pl.when(two == 0)
                        def _():
                            send(c, j // 2 - 1).start()

                    put(j).start()
                    return carry

                lax.fori_loop(0, steps, step, 0)
                put(steps - 1).wait()
                send(c, groups - 1).start()

            def give(job, r, n):
                g = n // per
                return pltpu.make_async_remote_copy(
                    ysend.at[n, :r], yrecv[job].at[n], ys_sem.at[n], yr_sem.at[job, n],
                    device_id={"b": mate(g)}, device_id_type=MESH,
                )

            def each(count, f):
                def one(n, carry):
                    f(n)
                    return carry

                lax.fori_loop(0, count, one, 0)

            def finish(job):
                kind, c = jobs[job]
                r = HALVES[c]

                def take(n):
                    return pltpu.make_async_copy(yrecv[job].at[n], yin.at[n, :r], ysem.at[n])

                def arrive(n):
                    give(job, r, n).wait()
                    take(n).start()

                each(3 * per, arrive)
                each(3 * per, lambda n: take(n).wait())

                def block(n):
                    at = pl.ds(pl.multiple_of(n * RB, RB), RB)
                    for p in range(per):
                        cols = slice(p * TN, (p + 1) * TN)
                        total = ystash[at, cols]
                        for g in range(3):
                            total = total + yin[g * per + p, at].astype(F32)
                        yout[at, cols] = total.astype(BF16)

                each(r // RB, block)
                copy = pltpu.make_async_copy(yout.at[:r], out_ref.at[pl.ds(row(c, kind == "m"), r)], yosem)
                copy.start()
                copy.wait()

            def down_job(i, job, c, mine):
                r = HALVES[c]
                source = (hmine if mine else htheirs)[c]

                def hidden_in(g):
                    at = pl.ds(pl.multiple_of(g * TN, TN), TN)
                    return pltpu.make_async_copy(source.at[g], lhs.at[:r, at], lsem.at[0])

                def load(g):
                    if not mine:
                        send_hidden(c, g).wait_recv()
                    hidden_in(g).start()

                each(groups, load)
                each(groups, lambda g: hidden_in(g).wait())

                def compute(j):
                    slot = lax.rem(base[i] + j, NW)
                    prefetch(i, j)
                    for copy in weights(i, j, slot):
                        copy.wait()
                    gu[:r] = jnp.dot(lhs[:r], w[slot], preferred_element_type=F32)

                def part(j):
                    compute(j)
                    ysend[j, :r] = gu[:r].astype(BF16)
                    give(job, r, j).start()

                def own(j):
                    compute(j + 3 * per)
                    ystash[:r, pl.ds(pl.multiple_of(j * TN, TN), TN)] = gu[:r]

                if job:
                    finish(job - 1)
                each(3 * per, part)
                each(per, own)

            for i, (kind, c) in enumerate(plan):
                if kind in "TM":
                    gate_up(i, c, kind == "M")
                else:
                    down_job(i, jobs.index((kind, c)), c, kind == "m")
            finish(len(jobs) - 1)

            for c in range(chunks):
                pltpu.make_async_remote_copy(
                    ssend[c], srecv[c], ss_sem.at[c], sr_sem.at[c, 0], device_id={"a": other}, device_id_type=MESH
                ).wait_send()
                pltpu.make_async_remote_copy(
                    hmine[c], htheirs[c], hs_sem.at[c], hr_sem.at[c, 0], device_id={"a": other}, device_id_type=MESH
                ).wait_send()
            forward(0).wait_send()
            for g in range(3):
                sent = pl.ds(0, rows - HALVES[0] if g == 1 else rows)
                pltpu.make_async_remote_copy(
                    x_ref.at[sent], xg_ref.at[g, sent], xs_sem.at[g], xr_sem.at[g, 0, 0],
                    device_id={"b": mates[g]}, device_id_type=MESH,
                ).wait_send()

        def hbm(*shape):
            return jax.ShapeDtypeStruct(shape, BF16)

        outs = [hbm(rows, dx), hbm(3, rows, dx)]
        outs += [hbm(steps, r, TN) for r in HALVES] * 2
        outs += [hbm(groups, r, TN) for r in HALVES] * 2
        outs += [hbm(3 * per, HALVES[c], TN) for _, c in jobs]
        sem = pltpu.SemaphoreType.DMA
        result = pl.pallas_call(
            kernel,
            name="gated_mlp",
            out_shape=outs,
            in_specs=[pl.BlockSpec(memory_space=pl.ANY)] * 4,
            out_specs=[pl.BlockSpec(memory_space=pl.ANY)] * len(outs),
            scratch_shapes=[
                pltpu.VMEM((top, ff), BF16),
                pltpu.VMEM((NW, ff, TN), BF16),
                pltpu.VMEM((top, TN), F32),
                pltpu.VMEM((2, top, TN), BF16),
                pltpu.VMEM((2, top, TN), BF16),
                pltpu.VMEM((2, top, HT), BF16),
                pltpu.VMEM((3 * per, top, TN), BF16),
                pltpu.VMEM((top, dx), F32),
                pltpu.VMEM((3 * per, top, TN), BF16),
                pltpu.VMEM((top, dx), BF16),
                sem((2, NW)), sem((4,)), sem((2,)), sem((2,)), sem((3 * per,)), sem,
                sem, sem((3,)), sem((3, chunks, 2)),
                sem((chunks,)), sem((chunks, groups)),
                sem((chunks,)), sem((chunks, groups)),
                sem((3 * per,)), sem((len(jobs), 3 * per)),
            ],
            compiler_params=pltpu.CompilerParams(
                collective_id=0, has_side_effects=True, vmem_limit_bytes=67043328
            ),
        )(x, w_gate, w_up, w_down)
        return result[0]

    return jax.shard_map(
        body,
        mesh=mesh,
        in_specs=(P("dp", ("a", "b")), P("a", "b"), P("a", "b"), P("b", "a")),
        out_specs=P("dp", ("a", "b")),
        check_vma=False,
    )
```

time: 2210 us -> 1000 us (0.45)
  waiting for transfers between devices: 1600 us -> 0 us
  Pallas kernels: 0 us -> 998 us
  matrix products: 602 us -> 0 us
    dot_general x1 -> x0, waiting for transfers between devices: 1270 us -> none  [step(): gate, up = (jnp.dot(x, w_gate), jnp.dot(x, w_up))]
    pallas_call x0 -> x1, Pallas kernels: none -> 998 us  [body(): pl.pallas_call(kernel, name='gated_mlp', out_shape=outs, in_specs=[pl.Blo...]
    dot_general x3 -> x0, matrix products: 602 us -> none  [the longest x2 394 us: step(): gate, up = (jnp.dot(x, w_gate), jnp.dot(x, w_up))]
    unnamed x5 -> x0, waiting for transfers between devices: 328 us -> none
  transfers between devices with their start and end apart: 3 -> 0, of which waited for: 3 -> 0; matrix products, arithmetic and copies ran while one was open for 0% -> 0% of each run, Pallas kernels for 0% -> 0%
where the time goes in v2:
time: 1000 us
  Pallas kernels  998 us (100%)
    pallas_call x1, Pallas kernels, body(): pl.pallas_call(kernel, name='gated_mlp', out_shape=outs, in_specs=[pl.Blo...  998 us

profile of v2, /device:TPU:0, one launch (start us, length us, event | category | flops | bytes accessed | tf_op | source)
XLA Modules:
  0.0 1003.8 jit_solution(14356053270776508040)
XLA Ops:
  0.0 997.9 %gated_mlp.1 = (bf16[2048,1536]{1,0:T(8,128)(2,1)}, bf16[3,2048,1536]{2,1,0:T(8,128)(2,1)}, bf16[28,128,512]{2,1,0:T(8,128)(2,1)}, bf16[28,448,512]{2,1,0:T(8,12...) custom-call(bf16[2048,1536]{1,0:T(8,128)(2,1)} %x_ref.1, ...), custom_call_target="tpu_custom_call" | custom-call | tf_op jit(solution)/shard_map/gated_mlp/pallas_call | solution.py:314
  997.9 5.9 copy.6

commit v3 on v2

--- a/solution.py
+++ b/solution.py
@@ -8,11 +8,11 @@
 MESH = pl.DeviceIdType.MESH
 BF16, F32 = jnp.bfloat16, jnp.float32
 
-HALVES = (128, 448, 288, 160)
+HALVES = (128, 448, 304, 144)
 TN = 512
 HT = TN // 2
 NW = 5
-RB = 32
+RB = 16
 ORDER = ("T0", "T1", "T2", "T3", "M0", "M1", "m0", "m1", "M2", "m2", "M3", "m3", "t0", "t1", "t2", "t3")
 
 
@@ -127,10 +127,9 @@
                 for copy in copies:
                     copy.wait()
 
-            def send_partial(c, g):
-                at = pl.ds(2 * g, 2)
-                return pltpu.make_async_remote_copy(
-                    ssend[c].at[at], srecv[c].at[at], ss_sem.at[c], sr_sem.at[c, g],
+            def send_partial(c, j):
+                return pltpu.make_async_remote_copy(
+                    ssend[c].at[j], srecv[c].at[j], ss_sem.at[c], sr_sem.at[c, j],
                     device_id={"a": other}, device_id_type=MESH,
                 )
 
@@ -141,9 +140,8 @@
                 )
 
             def gate_up(i, c, mine):
-                r = HALVES[c]
+                r, early = HALVES[c], i == 0
                 load_x(c, mine)
-                send = send_hidden if mine else send_partial
 
                 def partial_in(j, slot):
                     return pltpu.make_async_copy(srecv[c].at[j], si.at[slot, :r], isem.at[slot])
@@ -165,9 +163,7 @@
                     if mine:
                         @pl.when(j + 1 < steps)
                         def _():
-                            @pl.when(two == 1)
-                            def _():
-                                send_partial(c, (j + 1) // 2).wait_recv()
+                            send_partial(c, j + 1).wait_recv()
                             partial_in(j + 1, 1 - two).start()
                     for copy in weights(i, j, slot):
                         copy.wait()
@@ -187,20 +183,32 @@
                     else:
                         so[two, :r] = both.astype(BF16)
 
+                    if early:
+                        put(j).start()
+                        put(j).wait()
+                        send_partial(c, j).start()
+                        return carry
+
                     @pl.when(j > 0)
                     def _():
                         put(j - 1).wait()
-
-                        @pl.when(two == 0)
-                        def _():
-                            send(c, j // 2 - 1).start()
+                        if mine:
+                            @pl.when(two == 0)
+                            def _():
+                                send_hidden(c, j // 2 - 1).start()
+                        else:
+                            send_partial(c, j - 1).start()
 
                     put(j).start()
                     return carry
 
                 lax.fori_loop(0, steps, step, 0)
-                put(steps - 1).wait()
-                send(c, groups - 1).start()
+                if not early:
+                    put(steps - 1).wait()
+                    if mine:
+                        send_hidden(c, groups - 1).start()
+                    else:
+                        send_partial(c, steps - 1).start()
 
             def give(job, r, n):
                 g = n // per
@@ -216,19 +224,29 @@
 
                 lax.fori_loop(0, count, one, 0)
 
-            def finish(job):
+            def put_out(job):
                 kind, c = jobs[job]
                 r = HALVES[c]
+                return pltpu.make_async_copy(yout.at[:r], out_ref.at[pl.ds(row(c, kind == "m"), r)], yosem)
+
+            def sent(job):
+                each(3 * per, lambda n: give(job, HALVES[jobs[job][1]], n).wait_send())
+
+            def finish(job):
+                r = HALVES[jobs[job][1]]
 
                 def take(n):
                     return pltpu.make_async_copy(yrecv[job].at[n], yin.at[n, :r], ysem.at[n])
 
                 def arrive(n):
-                    give(job, r, n).wait()
+                    give(job, r, n).wait_recv()
                     take(n).start()
 
                 each(3 * per, arrive)
                 each(3 * per, lambda n: take(n).wait())
+
+                if job:
+                    put_out(job - 1).wait()
 
                 def block(n):
                     at = pl.ds(pl.multiple_of(n * RB, RB), RB)
@@ -240,9 +258,7 @@
                         yout[at, cols] = total.astype(BF16)
 
                 each(r // RB, block)
-                copy = pltpu.make_async_copy(yout.at[:r], out_ref.at[pl.ds(row(c, kind == "m"), r)], yosem)
-                copy.start()
-                copy.wait()
+                put_out(job).start()
 
             def down_job(i, job, c, mine):
                 r = HALVES[c]
@@ -277,8 +293,10 @@
                     ystash[:r, pl.ds(pl.multiple_of(j * TN, TN), TN)] = gu[:r]
 
                 if job:
+                    sent(job - 1)
+                each(3 * per, part)
+                if job:
                     finish(job - 1)
-                each(3 * per, part)
                 each(per, own)
 
             for i, (kind, c) in enumerate(plan):
@@ -287,6 +305,8 @@
                 else:
                     down_job(i, jobs.index((kind, c)), c, kind == "m")
             finish(len(jobs) - 1)
+            put_out(len(jobs) - 1).wait()
+            sent(len(jobs) - 1)
 
             for c in range(chunks):
                 pltpu.make_async_remote_copy(
@@ -297,9 +317,9 @@
                 ).wait_send()
             forward(0).wait_send()
             for g in range(3):
-                sent = pl.ds(0, rows - HALVES[0] if g == 1 else rows)
+                part = pl.ds(0, rows - HALVES[0] if g == 1 else rows)
                 pltpu.make_async_remote_copy(
-                    x_ref.at[sent], xg_ref.at[g, sent], xs_sem.at[g], xr_sem.at[g, 0, 0],
+                    x_ref.at[part], xg_ref.at[g, part], xs_sem.at[g], xr_sem.at[g, 0, 0],
                     device_id={"b": mates[g]}, device_id_type=MESH,
                 ).wait_send()
 
@@ -330,7 +350,7 @@
                 pltpu.VMEM((top, dx), BF16),
                 sem((2, NW)), sem((4,)), sem((2,)), sem((2,)), sem((3 * per,)), sem,
                 sem, sem((3,)), sem((3, chunks, 2)),
-                sem((chunks,)), sem((chunks, groups)),
+                sem((chunks,)), sem((chunks, steps)),
                 sem((chunks,)), sem((chunks, groups)),
                 sem((3 * per,)), sem((len(jobs), 3 * per)),
             ],

time: 1000 us -> 999 us (level)
  no operation moved by 1% of the time
where the time goes in v3:
time: 999 us; the launch traced here: 998 us
  Pallas kernels  992 us (99%)
    pallas_call x1, Pallas kernels, body(): pl.pallas_call(kernel, name='gated_mlp', out_shape=outs, in_specs=[pl.Blo...  992 us

profile of v3, /device:TPU:0, one launch (start us, length us, event | category | flops | bytes accessed | tf_op | source)
XLA Modules:
  0.0 998.3 jit_solution(8705987713745373564)
XLA Ops:
  0.0 992.4 %gated_mlp.1 = (bf16[2048,1536]{1,0:T(8,128)(2,1)}, bf16[3,2048,1536]{2,1,0:T(8,128)(2,1)}, bf16[28,128,512]{2,1,0:T(8,128)(2,1)}, bf16[28,448,512]{2,1,0:T(8,12...) custom-call(bf16[2048,1536]{1,0:T(8,128)(2,1)} %x_ref.1, ...), custom_call_target="tpu_custom_call" | custom-call | tf_op jit(solution)/shard_map/gated_mlp/pallas_call | solution.py:334
  992.4 5.9 copy.6
